TPU v7x, 32 devices: a whole 2x2x4 slice. The times are simulated.
32 devices in a mesh: rep: 1, r: 8 (over y, z), s: 4 (over x, core).
Axes of the slice: x: 2, y: 2, z: 4, core: 2. Of those that a mesh axis runs over, the one named last changes fastest.
Arguments:
- x: bfloat16 [32, 4096, 640], P(('rep', 'r', 's'))
- dy: bfloat16 [32, 4096, 640], P(('rep', 'r', 's'))
- w_gate: bfloat16 [2, 640, 2560], P(None, 's')
- w_up: bfloat16 [2, 640, 2560], P(None, 's')
- w_down: bfloat16 [2, 2560, 640], P(None, 's')
Outputs:
- output 1: bfloat16 [32, 4096, 640], P(('rep', 'r', 's'))
- output 2: bfloat16 [2, 640, 2560], P('rep', 's')
- output 3: bfloat16 [2, 640, 2560], P('rep', 's')
- output 4: bfloat16 [2, 2560, 640], P('rep', 's')
All inputs are finite; a program needn't handle non-finite values.
Results may differ from a plain program's by a relative error of at most 0.018.
Values are sent between devices in bfloat16 or wider.
A program may use at most 2 GiB of HBM per device.

v0:
```python
import jax
import jax.numpy as jnp
from jax import lax
from jax.sharding import PartitionSpec as P

NAMES = ("w_gate", "w_up", "w_down")


def matmul(a, w):
    return jnp.dot(a, w, preferred_element_type=jnp.float32).astype(jnp.bfloat16)


def normed(h):
    wide = h.astype(jnp.float32)
    scale = lax.rsqrt(jnp.mean(wide**2, -1, keepdims=True) + 1e-6)
    return (wide * scale).astype(jnp.bfloat16)


def layer(h, w):
    a = normed(h)
    gate = jnp.dot(a, w["w_gate"], preferred_element_type=jnp.float32)
    up = jnp.dot(a, w["w_up"], preferred_element_type=jnp.float32)
    return h + matmul((jax.nn.silu(gate) * up).astype(jnp.bfloat16), w["w_down"])


def solution(mesh):
    def fetched(weights, number):
        return {name: lax.all_gather(w[number], "s", axis=0, tiled=True) for name, w in zip(NAMES, weights, strict=True)}

    def summed(term):
        return lax.psum(lax.psum_scatter(term, "s", scatter_dimension=0, tiled=True), "r")

    def step(x, dy, *weights):
        layers = weights[0].shape[0]
        h, inputs = x[0], []
        for number in range(layers):
            inputs.append(h)
            h = layer(h, fetched(weights, number))
        by_h, mine = dy[0], [None] * layers
        for number in reversed(range(layers)):
            _, back = jax.vjp(lambda w, h: layer(h, w), fetched(weights, number), inputs[number])
            by_w, by_h = back(by_h)
            mine[number] = [summed(by_w[name]) for name in NAMES]
        return (by_h[None], *(jnp.stack([mine[number][i] for number in range(layers)]) for i in range(3)))

    states, cut = P(("rep", "r", "s"), None, None), P(None, "s", None)
    return jax.shard_map(
        step,
        mesh=mesh,
        in_specs=(states, states) + (cut,) * 3,
        out_specs=(states,) + (P("rep", "s", None),) * 3,
        check_vma=False,
    )
```

profile of v0, /device:TPU:0, one launch (start us, length us, event | category | flops | bytes accessed | tf_op | source)
XLA Modules:
  0.0 802.1 jit_solution(10157399592830002071)
XLA Ops:
  12.7 2.7 fusion.66
  17.2 7.9 copy.10
  25.1 3.6 fusion.15
  29.3 8.0 copy.9
  37.3 4.6 all-gather.13.cloned.1.call-done
  41.9 26.5 %fusion.46 = f32[4096,2560]{1,0:T(8,128)} fusion(bf16[1,4096,640]{1,2,0:T(8,128)(2,1)} %copy.10, f32[4096]{0:T(1024)S(1)} %fusion.59, bf16[1,640,2560]{2,1,0:T(8,128)(2,1)} %all-gather.13.cloned.1.call-done), kind=kOutput, calls=%fused_computation.65 | convolution fusion | flops 13429637120 | bytes 50479104 | tf_op jit(solution)/shard_map/dot_general | solution.py:21
  68.4 4.0 all-gather.15.cloned.1.call-done
  72.5 41.1 %multiply_convert_fusion.1 = (bf16[4096,2560]{1,0:T(8,128)(2,1)}, f32[4096,2560]{1,0:T(8,128)}) fusion(f32[4096,2560]{1,0:T(8,128)} %fusion.46, bf16[1,640,2560]{2,1,0:T(8,128)(2,1)} %all-gather.15.cloned.1.call-done, bf16[1,4096,640]{1,2,0:T(8,128)(2,1)} %copy.10, f32[4096]{0:T(1024)S(1)} %fusion.59), kind=kOutput, calls=%fused_computation.13 | convolution fusion | flops 13492551680 | bytes 113393664 | tf_op jit(solution)/shard_map/dot_general | solution.py:22
  113.6 22.3 %fusion.18 = (f32[4096]{0:T(1024)S(1)}, bf16[4096,640]{0,1:T(8,128)(2,1)}) fusion(bf16[4096,2560]{1,0:T(8,128)(2,1)} %get-tuple-element.20, bf16[1,2560,640]{2,1,0:T(8,128)(2,1)} %all-gather.17.cloned.1.call-done, bf16[1,4096,640]{1,2,0:T(8,128)(2,1)} %copy.10), kind=kOutput, calls=%fused_computation.40 | convolution fusion | flops 13434875904 | bytes 34750464 | tf_op jit(solution)/shard_map/dot_general | solution.py:10
  136.6 22.7 %convolution_convert_fusion.1 = bf16[4096,2560]{1,0:T(8,128)(2,1)} fusion(bf16[1,4096,640]{2,1,0:T(8,128)(2,1)} %param.6, bf16[1,2560,640]{2,1,0:T(8,128)(2,1)} %all-gather.21.cloned.1.call-done), kind=kOutput, calls=%fused_computation.21 | convolution fusion | flops 13432258560 | bytes 29491200 | tf_op jit(solution)/shard_map/transpose(jvp())/dot_general | solution.py:10
  159.3 5.2 all-gather.23.cloned.1.call-done
  164.5 26.5 %fusion.38 = f32[4096,2560]{1,0:T(8,128)} fusion(bf16[4096,640]{0,1:T(8,128)(2,1)} %get-tuple-element.23, f32[4096]{0:T(1024)S(1)} %fusion.60, bf16[1,640,2560]{2,1,0:T(8,128)(2,1)} %all-gather.23.cloned.1.call-done), kind=kOutput, calls=%fused_computation.62 | convolution fusion | flops 13429637120 | bytes 50479104 | tf_op jit(solution)/shard_map/jvp()/dot_general | solution.py:22
  191.0 4.5 all-gather.19.cloned.1.call-done
  195.5 59.5 %fusion.1 = (bf16[4096,2560]{1,0:T(8,128)(2,1)}, f32[4096,2560]{1,0:T(8,128)}) fusion(f32[4096,2560]{1,0:T(8,128)} %fusion.38, bf16[4096,2560]{1,0:T(8,128)(2,1)} %convolution_convert_fusion.1, bf16[1,640,2560]{2,1,0:T(8,128)(2,1)} %all-gather.19.cloned.1.call-done, bf16[4096,640]{0,1:T(8,128)(2,1)} %get-tuple-element.23, f32[4096]{0:T(1024)S(1)} %fusion.60), kind=kOutput, calls=%fused_computation.7 | convolution fusion | flops 13555466240 | bytes 134365184 | tf_op jit(solution)/shard_map/jvp()/dot_general | solution.py:21
  255.0 20.5 %convolution_convert_fusion.3 = bf16[4096,640]{0,1:T(8,128)(2,1)} fusion(bf16[4096,2560]{1,0:T(8,128)(2,1)} %get-tuple-element.24, bf16[1,640,2560]{2,1,0:T(8,128)(2,1)} %all-gather.19.cloned.1.call-done), kind=kOutput, calls=%fused_computation.46 | convolution fusion | flops 13421772800 | bytes 29491200 | tf_op jit(solution)/shard_map/transpose(jvp())/dot_general | solution.py:21
  275.5 28.6 %fusion.20 = (f32[4096]{0:T(1024)S(1)}, bf16[4096,640]{0,1:T(8,128)(2,1)}) fusion(bf16[4096,640]{0,1:T(8,128)(2,1)} %get-tuple-element.23, bf16[4096,640]{0,1:T(8,128)(2,1)} %convolution_convert_fusion.3, bf16[1,640,2560]{2,1,0:T(8,128)(2,1)S(1)} %copy-done.9, bf16[4096,2560]{1,0:T(8,128)(2,1)} %convolution_convert_fusion.1, f32[4096,2560]{1,0:T(8,128)} %get-tuple-element.25), kind=kOutput, calls=%fused_computation.42 | convolution fusion | flops 13500411904 | bytes 81936384 | tf_op jit(solution)/shard_map/transpose(jvp())/dot_general | solution.py:22
  304.2 11.9 %fusion.28 = bf16[4096,640]{0,1:T(8,128)(2,1)} fusion(bf16[4096,640]{0,1:T(8,128)(2,1)} %get-tuple-element.23, bf16[4096,640]{0,1:T(8,128)(2,1)} %get-tuple-element.27, bf16[1,4096,640]{1,2,0:T(8,128)(2,1)} %copy.9, f32[4096]{0:T(1024)S(1)} %multiply_multiply_fusion.1, f32[4096]{0:T(1024)S(1)} %fusion.60), kind=kLoop, calls=%fused_computation.53 | loop fusion | flops 18350080 | bytes 21004288 | tf_op jit(solution)/shard_map/transpose(jvp())/add_any | solution.py:14
  316.0 22.1 %convolution_convert_fusion.7 = bf16[2560,640]{1,0:T(8,128)(2,1)} fusion(bf16[4096,2560]{1,0:T(8,128)(2,1)} %get-tuple-element.20, bf16[4096,640]{0,1:T(8,128)(2,1)} %fusion.28), kind=kOutput, calls=%fused_computation.60 | convolution fusion | flops 13423411200 | bytes 29491200 | tf_op jit(solution)/shard_map/transpose(jvp())/dot_general | solution.py:10
  338.2 33.7 %fusion.33 = bf16[2560,640]{1,0:T(8,128)(2,1)} fusion(bf16[1,4096,640]{2,1,0:T(8,128)(2,1)} %param.6, f32[4096,2560]{1,0:T(8,128)} %fusion.38, f32[4096,2560]{1,0:T(8,128)} %get-tuple-element.25), kind=kOutput, calls=%fused_computation.61 | convolution fusion | flops 13486325760 | bytes 92405760 | tf_op jit(solution)/shard_map/transpose(jvp())/dot_general | solution.py:10
  371.9 50.4 %fusion.3 = (bf16[4096,2560]{1,0:T(8,128)(2,1)}, bf16[4096,2560]{1,0:T(8,128)(2,1)}) fusion(f32[4096,2560]{1,0:T(8,128)} %fusion.46, f32[4096,2560]{1,0:T(8,128)} %get-tuple-element.21, bf16[4096,640]{0,1:T(8,128)(2,1)} %fusion.28, bf16[1,2560,640]{2,1,0:T(8,128)(2,1)} %all-gather.17.cloned.1.call-done), kind=kOutput, calls=%fused_computation.9 | convolution fusion | flops 13558087680 | bytes 134348800 | tf_op jit(solution)/shard_map/transpose(jvp())/dot_general | solution.py:10
  422.4 27.3 %fusion.31 = bf16[640,2560]{1,0:T(8,128)(2,1)} fusion(bf16[4096,2560]{1,0:T(8,128)(2,1)} %get-tuple-element.29, bf16[1,4096,640]{1,2,0:T(8,128)(2,1)S(1)} %copy-done, f32[4096]{0:T(1024)S(1)} %copy-done.4, f32[4096,2560]{1,0:T(8,128)} %fusion.46), kind=kOutput, calls=%fused_computation.56 | convolution fusion | flops 13494190080 | bytes 71450624 | tf_op jit(solution)/shard_map/transpose(jvp())/dot_general | solution.py:22
  449.8 29.2 %fusion.32 = bf16[640,2560]{1,0:T(8,128)(2,1)} fusion(bf16[4096,2560]{1,0:T(8,128)(2,1)} %convolution_convert_fusion.1, bf16[4096,640]{0,1:T(8,128)(2,1)} %get-tuple-element.23, f32[4096]{0:T(1024)S(1)} %copy-done.6, f32[4096,2560]{1,0:T(8,128)} %get-tuple-element.25), kind=kOutput, calls=%fused_computation.57 | convolution fusion | flops 13494190080 | bytes 71450624 | tf_op jit(solution)/shard_map/transpose(jvp())/dot_general | solution.py:22
  479.0 20.6 %convolution_convert_fusion.5 = bf16[640,2560]{1,0:T(8,128)(2,1)} fusion(bf16[4096,2560]{1,0:T(8,128)(2,1)} %get-tuple-element.24, bf16[4096,640]{0,1:T(8,128)(2,1)} %get-tuple-element.23, f32[4096]{0:T(1024)S(1)} %copy-done.6), kind=kOutput, calls=%fused_computation.58 | convolution fusion | flops 13429637120 | bytes 29507584 | tf_op jit(solution)/shard_map/transpose(jvp())/dot_general | solution.py:21
  499.7 20.7 %convolution_convert_fusion.6 = bf16[640,2560]{1,0:T(8,128)(2,1)} fusion(bf16[4096,2560]{1,0:T(8,128)(2,1)} %get-tuple-element.28, bf16[1,4096,640]{1,2,0:T(8,128)(2,1)} %copy.10, f32[4096]{0:T(1024)S(1)} %copy-done.4), kind=kOutput, calls=%fused_computation.59 | convolution fusion | flops 13429637120 | bytes 29507584 | tf_op jit(solution)/shard_map/transpose(jvp())/dot_general | solution.py:21
  520.5 20.7 %convolution_convert_fusion.2 = bf16[4096,640]{0,1:T(8,128)(2,1)} fusion(bf16[4096,2560]{1,0:T(8,128)(2,1)} %get-tuple-element.28, bf16[1,640,2560]{2,1,0:T(8,128)(2,1)} %all-gather.13.cloned.1.call-done), kind=kOutput, calls=%fused_computation.45 | convolution fusion | flops 13421772800 | bytes 29491200 | tf_op jit(solution)/shard_map/transpose(jvp())/dot_general | solution.py:21
  541.2 28.5 %reduce-scatter.9.cloned.1.call-done = bf16[160,2560]{1,0:T(8,128)(2,1)} async-done(((bf16[640,2560]{1,0:T(8,128)(2,1)}), bf16[160,2560]{1,0:T(8,128)(2,1)}) %reduce-scatter.9.cloned.1.call-update) | async-done | bytes 819216 | tf_op jit(solution)/shard_map/reduce_scatter | solution.py:31
  569.7 40.7 %reduce-scatter.7.cloned.1.call-done = bf16[160,2560]{1,0:T(8,128)(2,1)} async-done(((bf16[640,2560]{1,0:T(8,128)(2,1)}), bf16[160,2560]{1,0:T(8,128)(2,1)}) %reduce-scatter.7.cloned.1.call-update) | async-done | bytes 819216 | tf_op jit(solution)/shard_map/reduce_scatter | solution.py:31
  610.4 34.1 %fusion.17 = (f32[4096]{0:T(1024)S(1)}, bf16[4096,640]{0,1:T(8,128)(2,1)}) fusion(bf16[1,4096,640]{1,2,0:T(8,128)(2,1)} %copy.10, bf16[4096,640]{0,1:T(8,128)(2,1)} %convolution_convert_fusion.2, bf16[1,640,2560]{2,1,0:T(8,128)(2,1)} %all-gather.15.cloned.1.call-done, bf16[4096,2560]{1,0:T(8,128)(2,1)} %get-tuple-element.29, f32[4096,2560]{1,0:T(8,128)} %fusion.46), kind=kOutput, calls=%fused_computation.39 | convolution fusion | flops 13500411904 | bytes 81936384 | tf_op jit(solution)/shard_map/transpose(jvp())/dot_general | solution.py:22
  644.5 11.9 %fusion.27 = bf16[1,4096,640]{1,2,0:T(8,128)(2,1)} fusion(bf16[4096,640]{0,1:T(8,128)(2,1)} %fusion.28, bf16[4096,640]{0,1:T(8,128)(2,1)} %get-tuple-element.31, bf16[1,4096,640]{1,2,0:T(8,128)(2,1)} %copy.10, f32[4096]{0:T(1024)S(1)} %multiply_multiply_fusion, f32[4096]{0:T(1024)S(1)} %copy-done.4), kind=kLoop, calls=%fused_computation.52 | loop fusion | flops 18350080 | bytes 21004288 | tf_op jit(solution)/shard_map/broadcast_in_dim | solution.py:44
  656.4 7.8 copy.11
  664.2 124.3 %all-reduce.3.cloned.1.call-done = (bf16[1,160,2560]{2,1,0:T(8,128)(2,1)}, bf16[1,160,2560]{2,1,0:T(8,128)(2,1)}, bf16[1,160,2560]{2,1,0:T(8,128)(2,1)}, bf16[1,...) async-done(((bf16[1,160,2560]{2,1,0:T(8,128)(2,1)}, bf16[1,160,2560]{2,1,0:T(8,128)(2,1)}, bf16[1,160,2560]{2,1,0:T(8,128)(2,1)}, ...) | async-done | bytes 4915216 | tf_op jit(solution)/shard_map/psum | solution.py:31
  791.3 3.9 pad_maximum_fusion
  (59 shorter events, 11.7 us)
Async XLA Ops:
  7.2 34.7 %all-gather.13.cloned.1.call-start = ((), (), s32[]{:S(2)}) async-start(), calls=%async_computation.12 | async-start | bytes 4096000 | tf_op jit(solution)/shard_map/all_gather | solution.py:28
  9.9 62.6 %all-gather.15.cloned.1.call-start = ((), (), s32[]{:S(2)}) async-start(), calls=%async_computation.13 | async-start | bytes 4096000 | tf_op jit(solution)/shard_map/all_gather | solution.py:28
  12.6 100.9 %all-gather.17.cloned.1.call-start = ((), (), s32[]{:S(2)}) async-start(), calls=%async_computation.14 | async-start | bytes 4096000 | tf_op jit(solution)/shard_map/all_gather | solution.py:28
  15.5 121.1 %all-gather.21.cloned.1.call-start = ((), (), s32[]{:S(2)}) async-start(), calls=%async_computation.16 | async-start | bytes 4096000 | tf_op jit(solution)/shard_map/all_gather | solution.py:28
  16.0 148.5 %all-gather.23.cloned.1.call-start = ((), (), s32[]{:S(2)}) async-start(), calls=%async_computation.17 | async-start | bytes 4096000 | tf_op jit(solution)/shard_map/all_gather | solution.py:28
  16.6 178.9 %all-gather.19.cloned.1.call-start = ((), (), s32[]{:S(2)}) async-start(), calls=%async_computation.15 | async-start | bytes 4096000 | tf_op jit(solution)/shard_map/all_gather | solution.py:28
  17.2 524.0 %reduce-scatter.15.cloned.1.call-start = ((), (), s32[]{:S(2)}) async-start(), calls=%async_computation.10 | async-start | bytes 4096000 | tf_op jit(solution)/shard_map/reduce_scatter | solution.py:31
  28.7 0.6 copy-start.1
  29.3 43.1 %copy-start.3 = (f32[4096]{0:T(1024)}, f32[4096]{0:T(1024)S(1)}, u32[]{:S(2)}) copy-start(f32[4096]{0:T(1024)S(1)} %fusion.59) | copy-start | bytes 49156
  135.9 0.6 copy-start.7
  136.5 167.6 %copy-start.5 = (f32[4096]{0:T(1024)}, f32[4096]{0:T(1024)S(1)}, u32[]{:S(2)}) copy-start(f32[4096]{0:T(1024)S(1)} %fusion.60) | copy-start | bytes 49156
  255.0 20.5 %copy-start.9 = (bf16[1,640,2560]{2,1,0:T(8,128)(2,1)S(1)}, bf16[1,640,2560]{2,1,0:T(8,128)(2,1)}, u32[]{:S(2)}) copy-start(bf16[1,640,2560]{2,1,0:T(8,128)(2,1)} %all-gather.23.cloned.1.call-done) | copy-start | bytes 9830404
  275.5 28.6 %copy-start.8 = (f32[4096]{0:T(1024)S(1)}, f32[4096]{0:T(1024)}, u32[]{:S(2)}) copy-start(f32[4096]{0:T(1024)} %copy-done.7) | copy-start | bytes 49156
  338.1 203.0 %reduce-scatter.17.cloned.1.call-start = ((), (), s32[]{:S(2)}) async-start(), calls=%async_computation.11 | async-start | bytes 4096000 | tf_op jit(solution)/shard_map/reduce_scatter | solution.py:31
  371.9 169.3 %reduce-scatter.11.cloned.1.call-start = ((), (), s32[]{:S(2)}) async-start(), calls=%async_computation.8 | async-start | bytes 4096000 | tf_op jit(solution)/shard_map/reduce_scatter | solution.py:31
  371.9 50.4 %copy-start = (bf16[1,4096,640]{1,2,0:T(8,128)(2,1)S(1)}, bf16[1,4096,640]{1,2,0:T(8,128)(2,1)}, u32[]{:S(2)}) copy-start(bf16[1,4096,640]{1,2,0:T(8,128)(2,1)} %copy.10) | copy-start | bytes 15728644
  371.9 50.4 %copy-start.4 = (f32[4096]{0:T(1024)S(1)}, f32[4096]{0:T(1024)}, u32[]{:S(2)}) copy-start(f32[4096]{0:T(1024)} %copy-done.3) | copy-start | bytes 49156
  422.4 27.4 %copy-start.6 = (f32[4096]{0:T(1024)S(1)}, f32[4096]{0:T(1024)}, u32[]{:S(2)}) copy-start(f32[4096]{0:T(1024)} %copy-done.5) | copy-start | bytes 49156
  449.7 91.5 %reduce-scatter.13.cloned.1.call-start = ((), (), s32[]{:S(2)}) async-start(), calls=%async_computation.9 | async-start | bytes 4096000 | tf_op jit(solution)/shard_map/reduce_scatter | solution.py:31
  479.0 90.7 %reduce-scatter.9.cloned.1.call-start = ((), (), s32[]{:S(2)}) async-start(), calls=%async_computation.7 | async-start | bytes 4096000 | tf_op jit(solution)/shard_map/reduce_scatter | solution.py:31
  499.7 110.7 %reduce-scatter.7.cloned.1.call-start = ((), (), s32[]{:S(2)}) async-start(), calls=%async_computation.6 | async-start | bytes 4096000 | tf_op jit(solution)/shard_map/reduce_scatter | solution.py:31
  520.4 268.1 %all-reduce.3.cloned.1.call-start = ((), (), s32[]{:S(2)}) async-start(), calls=%async_computation.18 | async-start | bytes 9830400 | tf_op jit(solution)/shard_map/psum | solution.py:31
  610.4 34.1 %copy-start.2 = (f32[4096]{0:T(1024)S(1)}, f32[4096]{0:T(1024)}, u32[]{:S(2)}) copy-start(f32[4096]{0:T(1024)} %copy-done.1) | copy-start | bytes 49156
Sparse Core Ops, SparseCore 0:
  10.1 31.7 all-gather.12
  43.4 28.9 all-gather.14
  74.0 28.9 all-gather.16
  104.5 28.9 all-gather.20
  135.5 28.9 all-gather.22
  166.5 28.9 all-gather.18
  338.2 38.2 reduce-scatter.14
  379.1 38.2 reduce-scatter.16
  449.8 38.2 reduce-scatter.10
  490.5 38.2 reduce-scatter.12
  531.4 38.2 reduce-scatter.8
  572.1 38.2 reduce-scatter.6
  614.8 173.7 all-reduce.2
where the time goes:
time: 811 us; the launch traced here: 802 us
  matrix products  507 us (63%)
  waiting for transfers between devices  214 us (26%)
  other arithmetic  34 us (4%)
  local copies, waits for them, and re-layouts  33 us (4%)
  between operations  14.4 us (2%)
    dot_general x6, matrix products, layer(): up = jnp.dot(a, w['w_up'], preferred_element_type=jnp.float32)  187 us
    dot_general x6, matrix products, layer(): gate = jnp.dot(a, w['w_gate'], preferred_element_type=jnp.float32)  168 us
    dot_general x5, matrix products, matmul(): jnp.dot(a, w, preferred_element_type=jnp.float32).astype(jnp.bfloat16)  151 us
    psum x1, waiting for transfers between devices, summed(): lax.psum(lax.psum_scatter(term, 's', scatter_dimension=0, tiled=True), 'r')  124 us
    reduce_scatter x6, waiting for transfers between devices, summed(): lax.psum_scatter(term, 's', scatter_dimension=0, tiled=True)  69.2 us
    unnamed x23, local copies, waits for them, and re-layouts  24.9 us
    all_gather x6, waiting for transfers between devices, fetched(): lax.all_gather(w[number], 's', axis=0, tiled=True)  18.3 us
  transfers between devices with their start and end apart: 13, of which 7 were waited for; matrix products, arithmetic and copies ran while one was open for 52% of the time, Pallas kernels for 0%

commit v1 on v0

v1 whole, which is shorter than its diff:
```python
import functools

import jax
import jax.numpy as jnp
from jax import lax
from jax.experimental import pallas as pl
from jax.experimental.pallas import tpu as pltpu
from jax.sharding import PartitionSpec as P

T, D, FF = 4096, 640, 2560
R = 512
NR = T // R
F, C = 5, 512
Q = 2 * F
NS, NG = 4, 8
PIECE = 240
BF, F32 = jnp.bfloat16, jnp.float32
MB = 1 << 20
NT = (((1,), (1,)), ((), ()))


def dot(a, b):
    return jnp.dot(a, b, preferred_element_type=F32)


def dot_nt(a, b):
    return lax.dot_general(a, b, NT, preferred_element_type=F32)


def sigmoid(v):
    return 1.0 / (1.0 + jnp.exp(-v))


def scale_of(wide):
    return lax.rsqrt(jnp.mean(wide * wide, -1, keepdims=True) + 1e-6)


def forward_kernel(x_ref, wg_ref, wu_ref, wd_ref, h_ref, prod_ref):
    wide = x_ref[...].astype(F32)
    a = (wide * scale_of(wide)).astype(BF)
    for f in range(F):
        cols = pl.ds(f * C, C)
        gate = dot(a, wg_ref[:, cols])
        up = dot(a, wu_ref[:, cols])
        prod_ref[:, cols] = (gate * sigmoid(gate) * up).astype(BF)
    h_ref[...] = (wide + dot(prod_ref[...], wd_ref[...]).astype(BF).astype(F32)).astype(BF)


def forward(x, wg, wu, wd):
    whole = lambda shape: pl.BlockSpec(shape, lambda i: (0, 0), pipeline_mode=pl.Buffered(1))
    return pl.pallas_call(
        forward_kernel,
        grid=(NR,),
        in_specs=[pl.BlockSpec((R, D), lambda i: (i, 0)), whole((D, FF)), whole((D, FF)), whole((FF, D))],
        out_specs=pl.BlockSpec((R, D), lambda i: (i, 0)),
        out_shape=jax.ShapeDtypeStruct((T, D), BF),
        scratch_shapes=[pltpu.VMEM((R, FF), BF)],
        compiler_params=pltpu.CompilerParams(vmem_limit_bytes=50 * MB),
        cost_estimate=pl.CostEstimate(flops=6 * T * D * FF, bytes_accessed=20 * MB, transcendentals=0),
        name="forward",
    )(x, wg, wu, wd)


def backward_kernel(h1_ref, x_ref, dy_hbm, wg1, wu1, wd1, wg0, wu0, wd0,
                    dx_ref, out_hbm, ra_hbm, rb_hbm,
                    a_s, at_s, dy_s, dyt_s, da_s, accg, accu, accd, wg_s, wu_s, wd_s,
                    sa, sb, sc, va, vb,
                    w_sem, l_sem, sa_sem, ra_sem, sb_sem, rb_sem, sc_sem, rc_sem, own_sem):
    l, f, r = pl.program_id(0), pl.program_id(1), pl.program_id(2)
    q = l * F + f
    slot = lax.rem(q, 2)
    me_s, me_r = lax.axis_index("s"), lax.axis_index("r")
    rows = pl.ds(pl.multiple_of(r * R, R), R)

    def fetch(q, act):
        to = lax.rem(q, 2)
        fq = lax.rem(q, F)
        for layer, (wg, wu, wd) in enumerate(((wg1, wu1, wd1), (wg0, wu0, wd0))):
            @pl.when(q // F == layer)
            def _():
                for s in range(NS):
                    units = pl.ds(pl.multiple_of(640 * s + 128 * fq, 128), 128)
                    here = pl.ds(128 * s, 128)
                    act(pltpu.make_async_copy(wg.at[:, units], wg_s.at[to, :, here], w_sem.at[to, 0, s]))
                    act(pltpu.make_async_copy(wu.at[:, units], wu_s.at[to, :, here], w_sem.at[to, 1, s]))
                    act(pltpu.make_async_copy(wd.at[units], wd_s.at[to, here], w_sem.at[to, 2, s]))

    def a_copy(q, k):
        to = lax.rem(me_s + k, NS)
        return pltpu.make_async_remote_copy(sa.at[lax.rem(q, 2), to], ra_hbm.at[q, k - 1], sa_sem.at[lax.rem(q, 2), k - 1], ra_sem.at[q, k - 1],
                                            device_id={"s": to}, device_id_type=pl.DeviceIdType.MESH)

    def b_copy(q, k):
        to = lax.rem(me_r + k, NG)
        return pltpu.make_async_remote_copy(sb.at[lax.rem(q, 2), to], rb_hbm.at[q, k - 1], sb_sem.at[lax.rem(q, 2), k - 1], rb_sem.at[q, k - 1],
                                            device_id={"r": to}, device_id_type=pl.DeviceIdType.MESH)

    def c_copy(q, k):
        to = lax.rem(me_r + k, NG)
        return pltpu.make_async_remote_copy(sc.at[lax.rem(q, 2)], out_hbm.at[q, me_r], sc_sem.at[lax.rem(q, 2), k - 1], rc_sem.at[q, k - 1],
                                            device_id={"r": to}, device_id_type=pl.DeviceIdType.MESH)

    def own_copy(q):
        return pltpu.make_async_copy(sc.at[lax.rem(q, 2)], out_hbm.at[q, me_r], own_sem.at[lax.rem(q, 2)])

    def pack(q):
        to = lax.rem(q, 2)
        @pl.when(q >= 2)
        def _():
            for k in range(1, NS):
                a_copy(q - 2, k).wait_send()
        for s in range(NS):
            for j in range(NS):
                for b in range(6):
                    if b < 2:
                        v = accg[160 * s + 80 * b:160 * s + 80 * b + 80, 128 * j:128 * j + 128]
                    elif b < 4:
                        v = accu[160 * s + 80 * (b - 2):160 * s + 80 * (b - 2) + 80, 128 * j:128 * j + 128]
                    else:
                        v = accd[160 * j + 80 * (b - 4):160 * j + 80 * (b - 4) + 80, 128 * s:128 * s + 128]
                    at = 80 * (b % 3)
                    sa[to, s, 2 * j + b // 3, at:at + 80, :] = v.astype(BF)
        for k in range(1, NS):
            a_copy(q, k).start()

    def a_load(q):
        for k in range(1, NS):
            a_copy(q, k).wait_recv()
        pltpu.make_async_copy(ra_hbm.at[q], va, l_sem.at[0]).start()

    def a_add(q):
        to = lax.rem(q, 2)
        pltpu.make_async_copy(ra_hbm.at[q], va, l_sem.at[0]).wait()
        @pl.when(q >= 2)
        def _():
            for k in range(1, NG):
                b_copy(q - 2, k).wait_send()
        @pl.loop(0, NG)
        def _(p):
            total = sa[to, me_s, p].astype(F32)
            for k in range(NS - 1):
                total += va[k, p].astype(F32)
            sb[to, p] = total.astype(BF)
        for k in range(1, NG):
            b_copy(q, k).start()

    def b_load(q):
        for k in range(1, NG):
            b_copy(q, k).wait_recv()
        pltpu.make_async_copy(rb_hbm.at[q], vb, l_sem.at[1]).start()

    def b_add(q):
        to = lax.rem(q, 2)
        pltpu.make_async_copy(rb_hbm.at[q], vb, l_sem.at[1]).wait()
        @pl.when(q >= 2)
        def _():
            for k in range(1, NG):
                c_copy(q - 2, k).wait_send()
            own_copy(q - 2).wait()
        total = sb[to, me_r].astype(F32)
        for k in range(NG - 1):
            total += vb[k].astype(F32)
        sc[to] = total.astype(BF)
        own_copy(q).start()
        for k in range(1, NG):
            c_copy(q, k).start()

    @pl.when((q == 0) & (r == 0))
    def _():
        fetch(q, lambda c: c.start())
        whole_dy = pltpu.make_async_copy(dy_hbm, dy_s, l_sem.at[2])
        whole_dy.start()
        barrier = pltpu.get_barrier_semaphore()
        for k in range(1, NS):
            pl.semaphore_signal(barrier, inc=1, device_id={"s": lax.rem(me_s + k, NS)}, device_id_type=pl.DeviceIdType.MESH)
        for k in range(1, NG):
            pl.semaphore_signal(barrier, inc=1, device_id={"r": lax.rem(me_r + k, NG)}, device_id_type=pl.DeviceIdType.MESH)
        pl.semaphore_wait(barrier, NS + NG - 2)
        whole_dy.wait()

    @pl.when(r == 0)
    def _():
        fetch(q, lambda c: c.wait())
        accg[...] = jnp.zeros_like(accg)
        accu[...] = jnp.zeros_like(accu)
        accd[...] = jnp.zeros_like(accd)

    @pl.when((r == 1) & (q < Q - 1))
    def _():
        fetch(q + 1, lambda c: c.start())

    @pl.when(f == 0)
    def _():
        wide = jnp.where(l == 0, h1_ref[...], x_ref[...]).astype(F32)
        a = (wide * scale_of(wide)).astype(BF)
        a_s[rows] = a
        at_s[:, rows] = a.T
        da_s[rows] = jnp.zeros((R, D), F32)

    @pl.when(q == 0)
    def _():
        dyt_s[:, rows] = dy_s[rows].T

    a = a_s[rows]
    wg, wu, wd = wg_s[slot], wu_s[slot], wd_s[slot]
    gate = dot(a, wg)
    up = dot(a, wu)
    by_prod = dot_nt(dy_s[rows], wd).astype(BF).astype(F32)
    sig = sigmoid(gate)
    silu = gate * sig
    prod = (silu * up).astype(BF)
    by_up = (by_prod * silu).astype(BF)
    by_gate = (by_prod * up * (sig + silu * (1.0 - sig))).astype(BF)
    accd[...] += dot(dyt_s[:, rows], prod)
    at = at_s[:, rows]
    accg[...] += dot(at, by_gate)
    accu[...] += dot(at, by_up)
    da_s[rows] += dot_nt(by_gate, wg) + dot_nt(by_up, wu)

    @pl.when(f == F - 1)
    def _():
        wide = jnp.where(l == 0, h1_ref[...], x_ref[...]).astype(F32)
        scale = scale_of(wide)
        unit = wide * scale
        da = da_s[rows]
        by_wide = scale * (da - unit * jnp.mean(da * unit, -1, keepdims=True))
        by_h = (dy_s[rows].astype(F32) + by_wide.astype(BF).astype(F32)).astype(BF)
        dx_ref[...] = by_h
        dy_s[rows] = by_h
        dyt_s[:, rows] = by_h.T

    @pl.when((r == 6) & (q >= 1))
    def _():
        a_load(q - 1)

    @pl.when((r == 7) & (q >= 1))
    def _():
        a_add(q - 1)

    @pl.when(r == 7)
    def _():
        pack(q)

    @pl.when((r == 3) & (q >= 2))
    def _():
        b_load(q - 2)

    @pl.when((r == 4) & (q >= 2))
    def _():
        b_add(q - 2)

    @pl.when((q == Q - 1) & (r == NR - 1))
    def _():
        b_load(Q - 2)
        b_add(Q - 2)
        a_load(Q - 1)
        a_add(Q - 1)
        b_load(Q - 1)
        b_add(Q - 1)
        for last in (Q - 2, Q - 1):
            for k in range(1, NS):
                a_copy(last, k).wait_send()
            for k in range(1, NG):
                b_copy(last, k).wait_send()
                c_copy(last, k).wait_send()
            own_copy(last).wait()
        @pl.loop(0, Q)
        def _(each):
            for k in range(1, NG):
                c_copy(each, k).wait_recv()


def backward(h1, x, dy, w1, w0):
    hbm = pl.BlockSpec(memory_space=pl.ANY)

    def tile(layer):
        def at(l, f, r):
            here = (l == layer) & ((f == 0) | (f == F - 1))
            return jnp.where(here, r, jnp.where(l >= layer, NR - 1, 0)), 0
        return at

    def last(l, f, r):
        return jnp.where((l == 1) & (f == F - 1), r, 0), 0

    dma = pltpu.SemaphoreType.DMA
    dx, out, _, _ = pl.pallas_call(
        backward_kernel,
        grid=(2, F, NR),
        in_specs=[pl.BlockSpec((R, D), tile(0)), pl.BlockSpec((R, D), tile(1))] + [hbm] * 7,
        out_specs=[pl.BlockSpec((R, D), last), hbm, hbm, hbm],
        out_shape=[
            jax.ShapeDtypeStruct((T, D), BF),
            jax.ShapeDtypeStruct((Q, NG, PIECE, 128), BF),
            jax.ShapeDtypeStruct((Q, NS - 1, NG, PIECE, 128), BF),
            jax.ShapeDtypeStruct((Q, NG - 1, PIECE, 128), BF),
        ],
        scratch_shapes=[
            pltpu.VMEM((T, D), BF), pltpu.VMEM((D, T), BF), pltpu.VMEM((T, D), BF), pltpu.VMEM((D, T), BF),
            pltpu.VMEM((T, D), F32),
            pltpu.VMEM((D, C), F32), pltpu.VMEM((D, C), F32), pltpu.VMEM((D, C), F32),
            pltpu.VMEM((2, D, C), BF), pltpu.VMEM((2, D, C), BF), pltpu.VMEM((2, C, D), BF),
            pltpu.VMEM((2, NS, NG, PIECE, 128), BF), pltpu.VMEM((2, NG, PIECE, 128), BF), pltpu.VMEM((2, PIECE, 128), BF),
            pltpu.VMEM((NS - 1, NG, PIECE, 128), BF), pltpu.VMEM((NG - 1, PIECE, 128), BF),
            dma((2, 3, NS)), dma((3,)), dma((2, NS - 1)), dma((Q, NS - 1)), dma((2, NG - 1)), dma((Q, NG - 1)),
            dma((2, NG - 1)), dma((Q, NG - 1)), dma((2,)),
        ],
        compiler_params=pltpu.CompilerParams(
            dimension_semantics=("arbitrary",) * 3, vmem_limit_bytes=63 * MB, collective_id=1, has_side_effects=True),
        cost_estimate=pl.CostEstimate(flops=32 * T * D * FF, bytes_accessed=100 * MB, transcendentals=0),
        name="backward",
    )(h1, x, dy, *w1, *w0)
    return dx, out


def solution(mesh):
    def gathered(w):
        return lax.all_gather(w, "s", axis=0, tiled=True)

    def step(x, dy, *weights):
        w0 = [gathered(w[0]) for w in weights]
        h1 = forward(x[0], *w0)
        w1 = [gathered(w[1]) for w in weights]
        dx, out = backward(h1, x[0], dy[0], w1, w0)
        sums = out.reshape(2, F, NS, 480, 128)[::-1]
        cut = lambda i: sums[:, :, :, 160 * i:160 * (i + 1)]
        wide = lambda v: v.transpose(0, 3, 2, 1, 4).reshape(2, 160, FF)
        down = cut(2).transpose(0, 1, 4, 2, 3).reshape(2, D, D)
        return dx[None], wide(cut(0)), wide(cut(1)), down

    states, cut = P(("rep", "r", "s"), None, None), P(None, "s", None)
    return jax.shard_map(
        step,
        mesh=mesh,
        in_specs=(states, states) + (cut,) * 3,
        out_specs=(states,) + (P("rep", "s", None),) * 3,
        check_vma=False,
    )
```

time: 811 us -> 611 us (0.75); the launches traced: 802 us -> 611 us
  matrix products: 507 us -> 0 us
  Pallas kernels: 0 us -> 435 us
  waiting for transfers between devices: 214 us -> 125 us
  other arithmetic: 34 us -> 0 us
    dot_general x17 -> x0, matrix products: 507 us -> none  [the longest x6 187 us: layer(): up = jnp.dot(a, w['w_up'], preferred_element_type=jnp.float32)]
    pallas_call x0 -> x2, Pallas kernels: none -> 435 us  [the longest x1 379 us: backward(): pl.pallas_call(backward_kernel, grid=(2, F, NR), in_specs=[pl.BlockSpec((...]
    psum x1 -> x0, waiting for transfers between devices: 124 us -> none  [summed(): lax.psum(lax.psum_scatter(term, 's', scatter_dimension=0, tiled=True), 'r')]
    all_gather x6, waiting for transfers between devices: 18.3 us -> 124 us  [gathered(): return lax.all_gather(w, 's', axis=0, tiled=True)]
    reduce_scatter x6 -> x0, waiting for transfers between devices: 69.2 us -> none  [summed(): lax.psum_scatter(term, 's', scatter_dimension=0, tiled=True)]
    broadcast_in_dim x1 -> x0, other arithmetic: 11.9 us -> none  [step(): by_h[None]]
    add_any x1 -> x0, other arithmetic: 11.9 us -> none  [normed(): wide = h.astype(jnp.float32)]
    reshape x0 -> x3, local copies, waits for them, and re-layouts: none -> 8.79 us  [the longest x2 5.79 us: step(): wide = lambda v: v.transpose(0, 3, 2, 1, 4).reshape(2, 160, FF)]
  transfers between devices with their start and end apart: 13 -> 6, of which waited for: 7 -> 5; matrix products, arithmetic and copies ran while one was open for 52% -> 0% of each run, Pallas kernels for 0% -> 9%
where the time goes in v1:
time: 611 us
  Pallas kernels  435 us (71%)
  waiting for transfers between devices  125 us (20%)
  local copies, waits for them, and re-layouts  36.6 us (6%)
  between operations  14.2 us (2%)
    pallas_call x1, Pallas kernels, backward(): pl.pallas_call(backward_kernel, grid=(2, F, NR), in_specs=[pl.BlockSpec((...  379 us
    all_gather x6, waiting for transfers between devices, gathered(): return lax.all_gather(w, 's', axis=0, tiled=True)  124 us
    pallas_call x1, Pallas kernels, forward(): pl.pallas_call(forward_kernel, grid=(NR,), in_specs=[pl.BlockSpec((R, D),...  55.4 us
    unnamed x13, local copies, waits for them, and re-layouts  16.5 us
  transfers between devices with their start and end apart: 6, of which 5 were waited for; matrix products, arithmetic and copies ran while one was open for 0% of the time, Pallas kernels for 9%

profile of v1, /device:TPU:0, one launch (start us, length us, event | category | flops | bytes accessed | tf_op | source)
XLA Modules:
  0.0 611.0 jit_solution(5123619850668153038)
XLA Ops:
  7.2 0.0 all-gather.13.cloned.1.call-start
  7.2 2.8 fusion.3
  10.0 0.0 all-gather.15.cloned.1.call-start
  10.1 1.3 fusion.2
  11.4 0.0 all-gather.17.cloned.1.call-start
  11.4 0.6 copy-done.3
  12.0 1.3 fusion.1
  13.4 0.0 all-gather.19.cloned.1.call-start
  13.4 0.5 all-gather.19.cloned.1.call-update
  14.0 0.5 all-gather.21.cloned.1.call-update
  14.5 0.0 all-gather.23.cloned.1.call-start
  14.6 0.5 all-gather.23.cloned.1.call-update
  15.1 26.8 %all-gather.13.cloned.1.call-done = bf16[1,640,2560]{2,1,0:T(8,128)(2,1)} async-done(((bf16[1,160,2560]{2,1,0:T(8,128)(2,1)}), bf16[1,640,2560]{2,1,0:T(8,128)(2,1)}) %all-gather.13.cloned.1.call-update) | async-done | bytes 3276816 | tf_op jit(solution)/shard_map/all_gather | solution.py:317
  41.9 31.2 %all-gather.15.cloned.1.call-done = bf16[1,640,2560]{2,1,0:T(8,128)(2,1)} async-done(((bf16[1,160,2560]{2,1,0:T(8,128)(2,1)}), bf16[1,640,2560]{2,1,0:T(8,128)(2,1)}) %all-gather.15.cloned.1.call-update) | async-done | bytes 3276816 | tf_op jit(solution)/shard_map/all_gather | solution.py:317
  73.1 30.6 %all-gather.17.cloned.1.call-done = bf16[1,2560,640]{2,1,0:T(8,128)(2,1)} async-done(((bf16[1,640,640]{2,1,0:T(8,128)(2,1)}), bf16[1,2560,640]{2,1,0:T(8,128)(2,1)}) %all-gather.17.cloned.1.call-update) | async-done | bytes 3276816 | tf_op jit(solution)/shard_map/all_gather | solution.py:317
  103.7 1.9 copy-done
  105.6 55.4 %forward.1.h1_ref = bf16[4096,640]{1,0:T(8,128)(2,1)} custom-call(bf16[4096,640]{1,0:T(8,128)(2,1)} %bitcast.22, bf16[640,2560]{1,0:T(8,128)(2,1)S(1)} %bitcast.19, bf16[640,2560]{1,0:T(8,128)(2,1)} %bitcast.25, bf16[2560,640]{1,0:T(8,128)(2,1)} %bitcast.27), custom_call_target="tpu_custom_call" | custom-call | flops 40265318400 | bytes 20971520 | tf_op jit(solution)/shard_map/forward/pallas_call | solution.py:51
  161.0 4.7 all-gather.21.cloned.1.call-done
  165.7 30.4 %all-gather.23.cloned.1.call-done = bf16[1,2560,640]{2,1,0:T(8,128)(2,1)} async-done(((bf16[1,640,640]{2,1,0:T(8,128)(2,1)}), bf16[1,2560,640]{2,1,0:T(8,128)(2,1)}) %all-gather.23.cloned.1.call-update) | async-done | bytes 3276816 | tf_op jit(solution)/shard_map/all_gather | solution.py:317
  196.1 379.2 %backward.1 = (bf16[4096,640]{1,0:T(8,128)(2,1)}, bf16[10,8,240,128]{3,2,1,0:T(8,128)(2,1)}, bf16[10,3,8,240,128]{4,3,2,1,0:T(8,128)(2,1)}, bf16[10,7,240,128]{3,2,1,0:T(8,128)(2,1)}) custom-call(bf16[4096,640]{1,0:T(8,128)(2,1)} %forward.1.h1_ref, bf16[4096,640]{1,0:T(8,128)(2,1)} %bitcast.23, bf16[4096,640]{1,0:T(8,128)(2,1)} %bitcast.24, ...), custom_call_target="tpu_custom_call" | custom-call | flops 214748364800 | bytes 104857600 | tf_op jit(solution)/shard_map/backward/pallas_call | solution.py:286
  575.3 4.7 fusion
  580.0 1.2 copy.18
  581.2 0.5 reverse_bitcast_fusion
  581.6 3.0 reshape.23
  584.6 3.7 copy.15
  588.3 1.2 copy.16
  589.5 0.5 reverse_bitcast_fusion.2
  590.0 2.9 reshape.21
  592.9 2.6 copy.17
  595.5 0.5 reverse_bitcast_fusion.1
  595.9 2.9 reshape.22
  598.8 5.3 copy.20
  (11 shorter events, 0.1 us)
Async XLA Ops:
  7.2 2.9 copy-start.2
  7.2 34.7 %all-gather.13.cloned.1.call-start = ((), (), s32[]{:S(2)}) async-start(), calls=%async_computation | async-start | bytes 4096000 | tf_op jit(solution)/shard_map/all_gather | solution.py:317
  10.0 2.0 copy-start.3
  10.0 63.1 %all-gather.15.cloned.1.call-start = ((), (), s32[]{:S(2)}) async-start(), calls=%async_computation.1 | async-start | bytes 4096000 | tf_op jit(solution)/shard_map/all_gather | solution.py:317
  11.4 92.3 %all-gather.17.cloned.1.call-start = ((), (), s32[]{:S(2)}) async-start(), calls=%async_computation.2 | async-start | bytes 4096000 | tf_op jit(solution)/shard_map/all_gather | solution.py:317
  13.4 147.7 %all-gather.19.cloned.1.call-start = ((), (), s32[]{:S(2)}) async-start(), calls=%async_computation.3 | async-start | bytes 4096000 | tf_op jit(solution)/shard_map/all_gather | solution.py:317
  13.9 151.7 %all-gather.21.cloned.1.call-start = ((), (), s32[]{:S(2)}) async-start(), calls=%async_computation.4 | async-start | bytes 4096000 | tf_op jit(solution)/shard_map/all_gather | solution.py:317
  14.5 181.6 %all-gather.23.cloned.1.call-start = ((), (), s32[]{:S(2)}) async-start(), calls=%async_computation.5 | async-start | bytes 4096000 | tf_op jit(solution)/shard_map/all_gather | solution.py:317
  103.7 1.9 copy-start
  584.6 3.7 copy-start.1
Sparse Core Ops, SparseCore 0:
  10.1 31.7 all-gather.12
  44.0 28.9 all-gather.14
  74.6 28.9 all-gather.16
  105.7 28.9 all-gather.18
  136.7 28.9 all-gather.20
  167.1 28.9 all-gather.22

commit v2 on v1

v2 whole, which is shorter than its diff:
```python
import functools

import jax
import jax.numpy as jnp
from jax import lax
from jax.experimental import pallas as pl
from jax.experimental.pallas import tpu as pltpu
from jax.sharding import PartitionSpec as P

T, D, FF = 4096, 640, 2560
R = 512
NR = T // R
F, C = 5, 512
Q = 2 * F
NS, NG = 4, 8
PIECE = 240
BF, F32 = jnp.bfloat16, jnp.float32
MB = 1 << 20
MESH = pl.DeviceIdType.MESH
NT = (((1,), (1,)), ((), ()))


def dot(a, b):
    return jnp.dot(a, b, preferred_element_type=F32)


def dot_nt(a, b):
    return lax.dot_general(a, b, NT, preferred_element_type=F32)


def sigmoid(v):
    return 1.0 / (1.0 + jnp.exp(-v))


def scale_of(wide):
    return lax.rsqrt(jnp.mean(wide * wide, -1, keepdims=True) + 1e-6)


def kernel(x_ref, dy_hbm, wg_in, wu_in, wd_in,
           dx_ref, out_hbm, ra_hbm, rb_hbm, h1_hbm, gg, gu, gd,
           a_s, at_s, dy_s, dyt_s, da_s, accg, accu, accd, wg_s, wu_s, wd_s,
           sa, sb, sc, va, vb, h_s,
           w_sem, l_sem, sa_sem, ra_sem, sb_sem, rb_sem, sc_sem, rc_sem, own_sem, h_sem, out_sem, in_sem):
    phase, f, r = pl.program_id(0), pl.program_id(1), pl.program_id(2)
    p = phase * F + f
    q = p - F
    slot = lax.rem(p, 2)
    me_s, me_r = lax.axis_index("s"), lax.axis_index("r")
    across = lax.rem(me_s + 2, NS)
    beside = me_s + 1 - 2 * lax.rem(me_s, 2)
    rows = pl.ds(pl.multiple_of(r * R, R), R)

    def mine(g):
        layer, part = g // F, lax.rem(g, F)
        for j in range(NS):
            units = pl.ds(pl.multiple_of(640 * j + 128 * part, 128), 128)
            yield 0, wg_in.at[layer, :, units], j
            yield 1, wu_in.at[layer, :, units], j
        yield 2, wd_in.at[layer, pl.ds(pl.multiple_of(128 * part, 128), 128)], 0

    def gather_send(g, way):
        to = across if way == 0 else beside
        owner = across if way == 2 else me_s
        if way == 2:
            pieces = [(m.at[g, owner], m.at[g, owner]) for m in (gg, gu, gd)]
        else:
            pieces = []
            for matrix, ref, j in mine(g):
                pieces.append((ref, gd.at[g, owner] if matrix == 2 else (gg, gu)[matrix].at[g, owner, :, pl.ds(128 * j, 128)]))
        for src, dst in pieces:
            pltpu.make_async_remote_copy(src, dst, out_sem.at[way, g], in_sem.at[way, g],
                                         device_id={"s": to}, device_id_type=MESH).start()

    def gather_wait(sem, g, way):
        pltpu.make_async_copy(ra_hbm.at[0, 0], ra_hbm.at[0, 0], sem.at[way, g]).wait()

    def relay(g):
        gather_wait(in_sem, g, 0)
        gather_send(g, 2)

    def fetch(p):
        to = lax.rem(p, 2)
        g = lax.rem(p, Q)
        for matrix, ref, j in mine(g):
            if matrix == 2:
                dst = wd_s.at[to, pl.ds(pl.multiple_of(128 * me_s, 128), 128)]
            else:
                dst = (wg_s, wu_s)[matrix].at[to, pl.ds(pl.multiple_of(160 * me_s, 32), 160), pl.ds(128 * j, 128)]
            pltpu.make_async_copy(ref, dst, w_sem.at[to, matrix]).start()
        for k in range(1, NS):
            s = lax.rem(me_s + k, NS)
            here = pl.ds(pl.multiple_of(160 * s, 32), 160)
            pltpu.make_async_copy(gg.at[g, s], wg_s.at[to, here], w_sem.at[to, 0]).start()
            pltpu.make_async_copy(gu.at[g, s], wu_s.at[to, here], w_sem.at[to, 1]).start()
            pltpu.make_async_copy(gd.at[g, s], wd_s.at[to, pl.ds(pl.multiple_of(128 * s, 128), 128)], w_sem.at[to, 2]).start()

    def fetched(p):
        to = lax.rem(p, 2)
        for matrix, w in enumerate((wg_s, wu_s, wd_s)):
            pltpu.make_async_copy(w.at[to], w.at[to], w_sem.at[to, matrix]).wait()

    def h_out(r):
        return pltpu.make_async_copy(h_s.at[lax.rem(r, 2)], h1_hbm.at[pl.ds(pl.multiple_of(r * R, R), R)], h_sem.at[lax.rem(r, 2)])

    def h_in(r):
        return pltpu.make_async_copy(h1_hbm.at[pl.ds(pl.multiple_of(r * R, R), R)], h_s.at[lax.rem(r, 2)], h_sem.at[lax.rem(r, 2)])


    def a_copy(q, k):
        to = lax.rem(me_s + k, NS)
        return pltpu.make_async_remote_copy(sa.at[lax.rem(q, 2), to], ra_hbm.at[q, k - 1], sa_sem.at[lax.rem(q, 2), k - 1], ra_sem.at[q, k - 1],
                                            device_id={"s": to}, device_id_type=MESH)

    def b_copy(q, k):
        to = lax.rem(me_r + k, NG)
        return pltpu.make_async_remote_copy(sb.at[lax.rem(q, 2), to], rb_hbm.at[q, k - 1], sb_sem.at[lax.rem(q, 2), k - 1], rb_sem.at[q, k - 1],
                                            device_id={"r": to}, device_id_type=MESH)

    def c_copy(q, k):
        to = lax.rem(me_r + k, NG)
        return pltpu.make_async_remote_copy(sc.at[lax.rem(q, 2)], out_hbm.at[q, me_r], sc_sem.at[lax.rem(q, 2), k - 1], rc_sem.at[q, k - 1],
                                            device_id={"r": to}, device_id_type=MESH)

    def own_copy(q):
        return pltpu.make_async_copy(sc.at[lax.rem(q, 2)], out_hbm.at[q, me_r], own_sem.at[lax.rem(q, 2)])

    def pack(q):
        to = lax.rem(q, 2)
        @pl.when(q >= 2)
        def _():
            for k in range(1, NS):
                a_copy(q - 2, k).wait_send()
        for s in range(NS):
            for j in range(NS):
                for b in range(6):
                    if b < 2:
                        v = accg[160 * s + 80 * b:160 * s + 80 * b + 80, 128 * j:128 * j + 128]
                    elif b < 4:
                        v = accu[160 * s + 80 * (b - 2):160 * s + 80 * (b - 2) + 80, 128 * j:128 * j + 128]
                    else:
                        v = accd[160 * j + 80 * (b - 4):160 * j + 80 * (b - 4) + 80, 128 * s:128 * s + 128]
                    at = 80 * (b % 3)
                    sa[to, s, 2 * j + b // 3, at:at + 80, :] = v.astype(BF)
        for k in range(1, NS):
            a_copy(q, k).start()

    def a_load(q):
        for k in range(1, NS):
            a_copy(q, k).wait_recv()
        pltpu.make_async_copy(ra_hbm.at[q], va, l_sem.at[0]).start()

    def a_add(q):
        to = lax.rem(q, 2)
        pltpu.make_async_copy(ra_hbm.at[q], va, l_sem.at[0]).wait()
        @pl.when(q >= 2)
        def _():
            for k in range(1, NG):
                b_copy(q - 2, k).wait_send()
        @pl.loop(0, NG)
        def _(p):
            total = sa[to, me_s, p].astype(F32)
            for k in range(NS - 1):
                total += va[k, p].astype(F32)
            sb[to, p] = total.astype(BF)
        for k in range(1, NG):
            b_copy(q, k).start()

    def b_load(q):
        for k in range(1, NG):
            b_copy(q, k).wait_recv()
        pltpu.make_async_copy(rb_hbm.at[q], vb, l_sem.at[1]).start()

    def b_add(q):
        to = lax.rem(q, 2)
        pltpu.make_async_copy(rb_hbm.at[q], vb, l_sem.at[1]).wait()
        @pl.when(q >= 2)
        def _():
            for k in range(1, NG):
                c_copy(q - 2, k).wait_send()
            own_copy(q - 2).wait()
        total = sb[to, me_r].astype(F32)
        for k in range(NG - 1):
            total += vb[k].astype(F32)
        sc[to] = total.astype(BF)
        own_copy(q).start()
        for k in range(1, NG):
            c_copy(q, k).start()

    whole_dy = pltpu.make_async_copy(dy_hbm, dy_s, l_sem.at[2])

    @pl.when((p == 0) & (r == 0))
    def _():
        barrier = pltpu.get_barrier_semaphore()
        for k in range(1, NS):
            pl.semaphore_signal(barrier, inc=1, device_id={"s": lax.rem(me_s + k, NS)}, device_id_type=MESH)
        for k in range(1, NG):
            pl.semaphore_signal(barrier, inc=1, device_id={"r": lax.rem(me_r + k, NG)}, device_id_type=MESH)
        pl.semaphore_wait(barrier, NS + NG - 2)
        for g in range(3):
            gather_send(g, 0)
            gather_send(g, 1)
        whole_dy.start()
        relay(0)
        gather_wait(in_sem, 0, 1)
        gather_wait(in_sem, 0, 2)
        fetch(0)

    @pl.when((r == 1) & (p < Q - 3))
    def _():
        gather_send(p + 3, 0)
        gather_send(p + 3, 1)

    @pl.when((r == 5) & (p < Q - 1))
    def _():
        relay(p + 1)

    @pl.when((r == 7) & (p < Q - 1))
    def _():
        gather_wait(in_sem, p + 1, 1)
        gather_wait(in_sem, p + 1, 2)

    @pl.when((r == 7) & (p < 3 * F - 1))
    def _():
        fetch(p + 1)

    @pl.when(r == 0)
    def _():
        fetched(p)

    @pl.when((r == 0) & (phase >= 1))
    def _():
        accg[...] = jnp.zeros_like(accg)
        accu[...] = jnp.zeros_like(accu)
        accd[...] = jnp.zeros_like(accd)

    def keep(wide):
        a = (wide * scale_of(wide)).astype(BF)
        a_s[rows] = a
        at_s[:, rows] = a.T

    @pl.when(f == 0)
    def _():
        da_s[rows] = jnp.zeros((R, D), F32)

    @pl.when((f == 0) & (phase != 1))
    def _():
        keep(x_ref[...].astype(F32))

    @pl.when((p == F) & (r == 0))
    def _():
        whole_dy.wait()
        h_out(NR - 2).wait()
        h_out(NR - 1).wait()

    @pl.when(p == F)
    def _():
        dyt_s[:, rows] = dy_s[rows].T

    @pl.when(phase == 0)
    def _():
        a = a_s[rows]
        gate = dot(a, wg_s[slot])
        up = dot(a, wu_s[slot])
        da_s[rows] += dot((gate * sigmoid(gate) * up).astype(BF), wd_s[slot])

    @pl.when(p == F - 1)
    def _():
        @pl.when(r >= 2)
        def _():
            h_out(r - 2).wait()
        h1 = (x_ref[...].astype(F32) + da_s[rows].astype(BF).astype(F32)).astype(BF)
        h_s[lax.rem(r, 2)] = h1
        keep(h1.astype(F32))
        h_out(r).start()

    @pl.when(phase >= 1)
    def _():
        a = a_s[rows]
        wg, wu, wd = wg_s[slot], wu_s[slot], wd_s[slot]
        gate = dot(a, wg)
        up = dot(a, wu)
        by_prod = dot_nt(dy_s[rows], wd).astype(BF).astype(F32)
        sig = sigmoid(gate)
        silu = gate * sig
        prod = (silu * up).astype(BF)
        by_up = (by_prod * silu).astype(BF)
        by_gate = (by_prod * up * (sig + silu * (1.0 - sig))).astype(BF)
        accd[...] += dot(dyt_s[:, rows], prod)
        at = at_s[:, rows]
        accg[...] += dot(at, by_gate)
        accu[...] += dot(at, by_up)
        da_s[rows] += dot_nt(by_gate, wg) + dot_nt(by_up, wu)

    def back(h):
        wide = h.astype(F32)
        scale = scale_of(wide)
        unit = wide * scale
        da = da_s[rows]
        by_wide = scale * (da - unit * jnp.mean(da * unit, -1, keepdims=True))
        return (dy_s[rows].astype(F32) + by_wide.astype(BF).astype(F32)).astype(BF)

    @pl.when((p == 2 * F - 2) & (r == NR - 1))
    def _():
        h_in(0).start()

    @pl.when(p == 2 * F - 1)
    def _():
        h_in(r).wait()
        @pl.when(r < NR - 1)
        def _():
            h_in(r + 1).start()
        by_h = back(h_s[lax.rem(r, 2)])
        dy_s[rows] = by_h
        dyt_s[:, rows] = by_h.T

    @pl.when(p == 3 * F - 1)
    def _():
        dx_ref[...] = back(x_ref[...])

    @pl.when((r == 6) & (q >= 1))
    def _():
        a_load(q - 1)

    @pl.when((r == 7) & (q >= 1))
    def _():
        a_add(q - 1)

    @pl.when((r == 7) & (q >= 0))
    def _():
        pack(q)

    @pl.when((r == 3) & (q >= 2))
    def _():
        b_load(q - 2)

    @pl.when((r == 4) & (q >= 2))
    def _():
        b_add(q - 2)

    @pl.when((q == Q - 1) & (r == NR - 1))
    def _():
        b_load(Q - 2)
        b_add(Q - 2)
        a_load(Q - 1)
        a_add(Q - 1)
        b_load(Q - 1)
        b_add(Q - 1)
        for last in (Q - 2, Q - 1):
            for k in range(1, NS):
                a_copy(last, k).wait_send()
            for k in range(1, NG):
                b_copy(last, k).wait_send()
                c_copy(last, k).wait_send()
            own_copy(last).wait()
        @pl.loop(0, Q)
        def _(each):
            for k in range(1, NG):
                c_copy(each, k).wait_recv()
            for way in range(3):
                gather_wait(out_sem, each, way)


def both_passes(x, dy, weights):
    hbm = pl.BlockSpec(memory_space=pl.ANY)

    def tile(phase, f, r):
        return jnp.where((phase != 1) & ((f == 0) | (f == F - 1)), r, NR - 1), 0

    def last(phase, f, r):
        return jnp.where((phase == 2) & (f == F - 1), r, 0), 0

    dma = pltpu.SemaphoreType.DMA
    dx, out, *_ = pl.pallas_call(
        kernel,
        grid=(3, F, NR),
        in_specs=[pl.BlockSpec((R, D), tile)] + [hbm] * 4,
        out_specs=[pl.BlockSpec((R, D), last)] + [hbm] * 7,
        out_shape=[
            jax.ShapeDtypeStruct((T, D), BF),
            jax.ShapeDtypeStruct((Q, NG, PIECE, 128), BF),
            jax.ShapeDtypeStruct((Q, NS - 1, NG, PIECE, 128), BF),
            jax.ShapeDtypeStruct((Q, NG - 1, PIECE, 128), BF),
            jax.ShapeDtypeStruct((T, D), BF),
            jax.ShapeDtypeStruct((Q, NS, 160, C), BF),
            jax.ShapeDtypeStruct((Q, NS, 160, C), BF),
            jax.ShapeDtypeStruct((Q, NS, 128, D), BF),
        ],
        scratch_shapes=[
            pltpu.VMEM((T, D), BF), pltpu.VMEM((D, T), BF), pltpu.VMEM((T, D), BF), pltpu.VMEM((D, T), BF),
            pltpu.VMEM((T, D), F32),
            pltpu.VMEM((D, C), F32), pltpu.VMEM((D, C), F32), pltpu.VMEM((D, C), F32),
            pltpu.VMEM((2, D, C), BF), pltpu.VMEM((2, D, C), BF), pltpu.VMEM((2, C, D), BF),
            pltpu.VMEM((2, NS, NG, PIECE, 128), BF), pltpu.VMEM((2, NG, PIECE, 128), BF), pltpu.VMEM((2, PIECE, 128), BF),
            pltpu.VMEM((NS - 1, NG, PIECE, 128), BF), pltpu.VMEM((NG - 1, PIECE, 128), BF), pltpu.VMEM((2, R, D), BF),
            dma((2, 3)), dma((3,)), dma((2, NS - 1)), dma((Q, NS - 1)), dma((2, NG - 1)), dma((Q, NG - 1)),
            dma((2, NG - 1)), dma((Q, NG - 1)), dma((2,)), dma((2,)), dma((3, Q)), dma((3, Q)),
        ],
        compiler_params=pltpu.CompilerParams(
            dimension_semantics=("arbitrary",) * 3, vmem_limit_bytes=63 * MB, collective_id=1, has_side_effects=True),
        cost_estimate=pl.CostEstimate(flops=38 * T * D * FF, bytes_accessed=100 * MB, transcendentals=0),
        name="both_passes",
    )(x, dy, *weights)
    return dx, out


def solution(mesh):
    def step(x, dy, *weights):
        dx, out = both_passes(x[0], dy[0], weights)
        sums = out.reshape(2, F, NS, 480, 128)[::-1]
        cut = lambda i: sums[:, :, :, 160 * i:160 * (i + 1)]
        wide = lambda v: v.transpose(0, 3, 2, 1, 4).reshape(2, 160, FF)
        down = cut(2).transpose(0, 1, 4, 2, 3).reshape(2, D, D)
        return dx[None], wide(cut(0)), wide(cut(1)), down

    states, cut = P(("rep", "r", "s"), None, None), P(None, "s", None)
    return jax.shard_map(
        step,
        mesh=mesh,
        in_specs=(states, states) + (cut,) * 3,
        out_specs=(states,) + (P("rep", "s", None),) * 3,
        check_vma=False,
    )
```

time: 611 us -> 508 us (0.83)
  waiting for transfers between devices: 125 us -> 0 us
  Pallas kernels: 435 us -> 478 us
  between operations: 14.2 us -> 0.67 us
  local copies, waits for them, and re-layouts: 36.6 us -> 28.7 us
    all_gather x6 -> x0, waiting for transfers between devices: 124 us -> none  [gathered(): return lax.all_gather(w, 's', axis=0, tiled=True)]
    pallas_call x2 -> x1, Pallas kernels: 435 us -> 478 us  [both_passes(): pl.pallas_call(kernel, grid=(3, F, NR), in_specs=[pl.BlockSpec((R, D), ti...]
    unnamed x13 -> x7, local copies, waits for them, and re-layouts: 16.5 us -> 13.9 us
  transfers between devices with their start and end apart: 6 -> 0, of which waited for: 5 -> 0; matrix products, arithmetic and copies ran while one was open for 0% -> 0% of each run, Pallas kernels for 9% -> 0%
where the time goes in v2:
time: 508 us; the launch traced here: 507 us
  Pallas kernels  478 us (94%)
  local copies, waits for them, and re-layouts  28.7 us (6%)
    pallas_call x1, Pallas kernels, both_passes(): pl.pallas_call(kernel, grid=(3, F, NR), in_specs=[pl.BlockSpec((R, D), ti...  478 us
    unnamed x7, local copies, waits for them, and re-layouts  13.9 us

profile of v2, /device:TPU:0, one launch (start us, length us, event | category | flops | bytes accessed | tf_op | source)
XLA Modules:
  0.0 507.4 jit_solution(17171246615174789752)
XLA Ops:
  0.6 477.9 %both_passes.1 = (bf16[4096,640]{1,0:T(8,128)(2,1)}, bf16[10,8,240,128]{3,2,1,0:T(8,128)(2,1)}, bf16[10,3,8,240,128]{4,3,2,1,0:T(8,128)(2,1)}, bf16[10,7,240,128...) custom-call(bf16[4096,640]{1,0:T(8,128)(2,1)} %bitcast.14, ...), custom_call_target="tpu_custom_call" | custom-call | flops 255013683200 | bytes 104857600 | tf_op jit(solution)/shard_map/both_passes/pallas_call | solution.py:373
  478.6 4.7 fusion
  483.2 1.2 copy.18
  484.4 0.5 reverse_bitcast_fusion
  484.9 3.0 reshape.23
  487.9 0.0 copy-start
  487.9 3.7 copy.15
  491.5 0.0 copy-done
  491.6 1.2 copy.16
  492.7 0.5 reverse_bitcast_fusion.2
  493.2 2.9 reshape.21
  496.1 2.6 copy.17
  498.7 0.5 reverse_bitcast_fusion.1
  499.2 2.9 reshape.22
  502.1 5.3 %copy.20 = bf16[1,4096,640]{2,1,0:T(8,128)(2,1)} copy(bf16[1,4096,640]{2,1,0:T(8,128)(2,1)} %bitcast.12) | data formatting | bytes 10485760
Async XLA Ops:
  487.9 3.7 copy-start

commit v3 on v2

v3 whole, which is shorter than its diff:
```python
import functools

import jax
import jax.numpy as jnp
from jax import lax
from jax.experimental import pallas as pl
from jax.experimental.pallas import tpu as pltpu
from jax.sharding import PartitionSpec as P

T, D, FF = 4096, 640, 2560
R = 512
NR = T // R
F, C = 5, 512
Q = 2 * F
NS, NG = 4, 8
BLOCK, PIECE = 1920, 240
BF, F32 = jnp.bfloat16, jnp.float32
MB = 1 << 20
MESH = pl.DeviceIdType.MESH
NT = (((1,), (1,)), ((), ()))


def dot(a, b):
    return jnp.dot(a, b, preferred_element_type=F32)


def dot_nt(a, b):
    return lax.dot_general(a, b, NT, preferred_element_type=F32)


def sigmoid(v):
    return 1.0 / (1.0 + jnp.exp(-v))


def scale_of(wide):
    return lax.rsqrt(jnp.mean(wide * wide, -1, keepdims=True) + 1e-6)


def kernel(x_hbm, dy_hbm, wg_in, wu_in, wd_in,
           dx_hbm, out_g, out_u, out_d, r1_hbm, r2_hbm, rb_hbm, h1_hbm, by_hbm, gg, gu, gd,
           a_s, at_s, dy_s, dyt_s, da_s, accg, accu, accd, wg_s, wu_s, wd_s,
           sa, sx, sb, sc, scd, v1, v2, vb, x_s, h_s, by_s,
           w_sem, l_sem, s1_sem, r1_sem, s2_sem, r2_sem, sb_sem, rb_sem, sc_sem, rc_sem, own_sem, x_sem, h_sem, by_sem, out_sem, in_sem):
    phase, f, r = pl.program_id(0), pl.program_id(1), pl.program_id(2)
    p = phase * F + f
    q = p - F
    slot = lax.rem(p, 2)
    me_s, me_r = lax.axis_index("s"), lax.axis_index("r")
    across = lax.rem(me_s + 2, NS)
    beside = me_s + 1 - 2 * lax.rem(me_s, 2)
    rows = pl.ds(pl.multiple_of(r * R, R), R)
    now = f * NR + r
    turn = lax.rem(r, 2)

    def mine(g):
        layer, part = g // F, lax.rem(g, F)
        for j in range(NS):
            units = pl.ds(pl.multiple_of(640 * j + 128 * part, 128), 128)
            yield 0, wg_in.at[layer, :, units], j
            yield 1, wu_in.at[layer, :, units], j
        yield 2, wd_in.at[layer, pl.ds(pl.multiple_of(128 * part, 128), 128)], 0

    def gather_send(g, way):
        to = across if way == 0 else beside
        owner = across if way == 2 else me_s
        if way == 2:
            pieces = [(m.at[g, owner], m.at[g, owner]) for m in (gg, gu, gd)]
        else:
            pieces = []
            for matrix, ref, j in mine(g):
                pieces.append((ref, gd.at[g, owner] if matrix == 2 else (gg, gu)[matrix].at[g, owner, :, pl.ds(128 * j, 128)]))
        for src, dst in pieces:
            pltpu.make_async_remote_copy(src, dst, out_sem.at[way, g], in_sem.at[way, g],
                                         device_id={"s": to}, device_id_type=MESH).start()

    def gather_wait(sem, g, way):
        pltpu.make_async_copy(r2_hbm.at[0], r2_hbm.at[0], sem.at[way, g]).wait()

    def relay(g):
        gather_wait(in_sem, g, 0)
        gather_send(g, 2)

    def fetch(p):
        to = lax.rem(p, 2)
        g = jnp.where(p < Q, p, lax.rem(p, F))
        for matrix, ref, j in mine(g):
            if matrix == 2:
                dst = wd_s.at[to, pl.ds(pl.multiple_of(128 * me_s, 128), 128)]
            else:
                dst = (wg_s, wu_s)[matrix].at[to, pl.ds(pl.multiple_of(160 * me_s, 32), 160), pl.ds(128 * j, 128)]
            pltpu.make_async_copy(ref, dst, w_sem.at[to, matrix]).start()
        for k in range(1, NS):
            s = lax.rem(me_s + k, NS)
            here = pl.ds(pl.multiple_of(160 * s, 32), 160)
            pltpu.make_async_copy(gg.at[g, s], wg_s.at[to, here], w_sem.at[to, 0]).start()
            pltpu.make_async_copy(gu.at[g, s], wu_s.at[to, here], w_sem.at[to, 1]).start()
            pltpu.make_async_copy(gd.at[g, s], wd_s.at[to, pl.ds(pl.multiple_of(128 * s, 128), 128)], w_sem.at[to, 2]).start()

    def fetched(p):
        to = lax.rem(p, 2)
        for matrix, w in enumerate((wg_s, wu_s, wd_s)):
            pltpu.make_async_copy(w.at[to], w.at[to], w_sem.at[to, matrix]).wait()

    def h_out(r):
        return pltpu.make_async_copy(h_s.at[lax.rem(r, 2)], h1_hbm.at[pl.ds(pl.multiple_of(r * R, R), R)], h_sem.at[lax.rem(r, 2)])

    def h_in(r):
        return pltpu.make_async_copy(h1_hbm.at[pl.ds(pl.multiple_of(r * R, R), R)], h_s.at[lax.rem(r, 2)], h_sem.at[lax.rem(r, 2)])


    def x_in(r):
        return pltpu.make_async_copy(x_hbm.at[pl.ds(pl.multiple_of(r * R, R), R)], x_s.at[lax.rem(r, 2)], x_sem.at[lax.rem(r, 2)])

    def x_tile():
        @pl.when(r < NR - 1)
        def _():
            x_in(r + 1).start()
        x_in(r).wait()
        return x_s[turn]

    def dx_out(r):
        return pltpu.make_async_copy(h_s.at[lax.rem(r, 2)], dx_hbm.at[pl.ds(pl.multiple_of(r * R, R), R)], h_sem.at[lax.rem(r, 2)])

    def by_out(t):
        return pltpu.make_async_copy(by_s.at[lax.rem(t, 2)], by_hbm.at[t], by_sem.at[lax.rem(t, 2)])

    def by_in(t):
        return pltpu.make_async_copy(by_hbm.at[t], by_s.at[lax.rem(t, 2)], by_sem.at[lax.rem(t, 2)])

    def s1_copy(q, i):
        to = beside if i == 0 else lax.rem(beside + 2, NS)
        return pltpu.make_async_remote_copy(sa.at[lax.rem(q, 2), to], r1_hbm.at[q, i], s1_sem.at[lax.rem(q, 2), i], r1_sem.at[q, i],
                                            device_id={"s": beside}, device_id_type=MESH)

    def s2_copy(q):
        return pltpu.make_async_remote_copy(sx, r2_hbm.at[q], s2_sem.at[0], r2_sem.at[q], device_id={"s": across}, device_id_type=MESH)

    def b_copy(q, k):
        to = lax.rem(me_r + k, NG)
        return pltpu.make_async_remote_copy(sb.at[lax.rem(q, 2), to], rb_hbm.at[q, k - 1], sb_sem.at[lax.rem(q, 2), k - 1], rb_sem.at[q, k - 1],
                                            device_id={"r": to}, device_id_type=MESH)

    def places(q):
        to, layer, part = lax.rem(q, 2), 1 - q // F, lax.rem(q, F)
        units = pl.ds(pl.multiple_of(640 * (me_r // 2) + 128 * part, 128), 128)
        some = pl.ds(pl.multiple_of(80 * lax.rem(me_r, 2), 16), 80)
        yield sc.at[to, 0], out_g.at[layer, some, units]
        yield sc.at[to, 1], out_u.at[layer, some, units]
        yield scd.at[to], out_d.at[layer, pl.ds(pl.multiple_of(128 * part + 16 * me_r, 16), 16)]

    def c_send(q):
        to = lax.rem(q, 2)
        for src, dst in places(q):
            pltpu.make_async_copy(src, dst, own_sem.at[to]).start()
            for k in range(1, NG):
                pltpu.make_async_remote_copy(src, dst, sc_sem.at[to, k - 1], rc_sem.at[q, k - 1],
                                             device_id={"r": lax.rem(me_r + k, NG)}, device_id_type=MESH).start()

    def c_wait(sem):
        pltpu.make_async_copy(rb_hbm.at[0, 0], rb_hbm.at[0, 0], sem).wait()

    def c_sent(q):
        to = lax.rem(q, 2)
        c_wait(own_sem.at[to])
        for k in range(1, NG):
            c_wait(sc_sem.at[to, k - 1])

    def pack(q):
        to = lax.rem(q, 2)
        @pl.when(q >= 2)
        def _():
            s1_copy(q - 2, 0).wait_send()
            s1_copy(q - 2, 1).wait_send()
        for s in range(NS):
            for j in range(NS):
                for h in range(2):
                    at = 160 * (2 * j + h)
                    here = slice(160 * s + 80 * h, 160 * s + 80 * h + 80), slice(128 * j, 128 * j + 128)
                    sa[to, s, at:at + 80] = accg[here].astype(BF)
                    sa[to, s, at + 80:at + 160] = accu[here].astype(BF)
            sa[to, s, 1280:] = accd[:, 128 * s:128 * s + 128].astype(BF)
        s1_copy(q, 0).start()
        s1_copy(q, 1).start()

    def s1_load(q):
        s1_copy(q, 0).wait_recv()
        s1_copy(q, 1).wait_recv()
        pltpu.make_async_copy(r1_hbm.at[q], v1, l_sem.at[0]).start()

    def s1_add(q):
        pltpu.make_async_copy(r1_hbm.at[q], v1, l_sem.at[0]).wait()
        @pl.when(q >= 1)
        def _():
            s2_copy(q - 1).wait_send()
        @pl.loop(0, 8)
        def _(p):
            at = pl.ds(pl.multiple_of(240 * p, 16), 240)
            sx[at] = (sa[lax.rem(q, 2), across, at].astype(F32) + v1[1, at].astype(F32)).astype(BF)
        s2_copy(q).start()

    def s2_load(q):
        s2_copy(q).wait_recv()
        pltpu.make_async_copy(r2_hbm.at[q], v2, l_sem.at[1]).start()

    def s2_add(q):
        to = lax.rem(q, 2)
        pltpu.make_async_copy(r2_hbm.at[q], v2, l_sem.at[1]).wait()
        @pl.when(q >= 2)
        def _():
            for k in range(1, NG):
                b_copy(q - 2, k).wait_send()
        def total(at):
            return (sa[to, me_s, at].astype(F32) + v1[0, at].astype(F32) + v2[at].astype(F32)).astype(BF)
        @pl.loop(0, NG)
        def _(p):
            sb[to, p, :160] = total(pl.ds(pl.multiple_of(160 * p, 32), 160))
        down = total(pl.ds(1280, 640)).T
        for p in range(NG):
            for t in range(5):
                sb[to, p, 160 + 16 * t:176 + 16 * t] = down[16 * p:16 * p + 16, 128 * t:128 * t + 128]
        for k in range(1, NG):
            b_copy(q, k).start()

    def b_load(q):
        for k in range(1, NG):
            b_copy(q, k).wait_recv()
        pltpu.make_async_copy(rb_hbm.at[q], vb, l_sem.at[2]).start()

    def b_add(q):
        to = lax.rem(q, 2)
        pltpu.make_async_copy(rb_hbm.at[q], vb, l_sem.at[2]).wait()
        @pl.when(q >= 2)
        def _():
            c_sent(q - 2)
        total = sb[to, me_r].astype(F32)
        for k in range(NG - 1):
            total += vb[k].astype(F32)
        total = total.astype(BF)
        sc[to, 0] = total[:80]
        sc[to, 1] = total[80:160]
        for t in range(5):
            scd[to, :, 128 * t:128 * t + 128] = total[160 + 16 * t:176 + 16 * t]
        c_send(q)

    whole_dy = pltpu.make_async_copy(dy_hbm, dy_s, l_sem.at[3])

    def keep(wide, rows):
        a = (wide * scale_of(wide)).astype(BF)
        a_s[rows] = a
        at_s[:, rows] = a.T

    def begin():
        barrier = pltpu.get_barrier_semaphore()
        x_in(0).start()
        for k in range(1, NS):
            pl.semaphore_signal(barrier, inc=1, device_id={"s": lax.rem(me_s + k, NS)}, device_id_type=MESH)
        for k in range(1, NG):
            pl.semaphore_signal(barrier, inc=1, device_id={"r": lax.rem(me_r + k, NG)}, device_id_type=MESH)
        pl.semaphore_wait(barrier, NS + NG - 2)
        for g in range(3):
            gather_send(g, 0)
            gather_send(g, 1)

        @pl.loop(0, NR)
        def _(i):
            @pl.when(i < NR - 1)
            def _():
                x_in(i + 1).start()
            x_in(i).wait()
            here = pl.ds(pl.multiple_of(i * R, R), R)
            keep(x_s[lax.rem(i, 2)].astype(F32), here)
            da_s[i] = jnp.zeros((D, R), F32)

        whole_dy.start()
        relay(0)
        gather_wait(in_sem, 0, 1)
        gather_wait(in_sem, 0, 2)
        fetch(0)

    def clear():
        accg[...] = jnp.zeros_like(accg)
        accu[...] = jnp.zeros_like(accu)
        accd[...] = jnp.zeros_like(accd)

    def weights_of_next():
        @pl.when(p < Q - 1)
        def _():
            gather_wait(in_sem, p + 1, 1)
            gather_wait(in_sem, p + 1, 2)
        pl.when(p < 4 * F - 1)(lambda: fetch(p + 1))
        pl.when((p == F - 2) | (p == 2 * F - 1) | (p == 4 * F - 2))(lambda: x_in(0).start())

    def send_later():
        gather_send(p + 3, 0)
        gather_send(p + 3, 1)

    @pl.when(r == 0)
    def _():
        pl.when(p == 0)(begin)
        fetched(p)
        pl.when((q >= 0) & (q < Q))(clear)

    @pl.when(((r == 1) | (r == 4)) & (p < Q - 1))
    def _():
        pl.when((r == 1) & (p < Q - 3))(send_later)
        pl.when(r == 4)(lambda: relay(p + 1))

    @pl.when(r == 6)
    def _():
        weights_of_next()

    @pl.when((f == 0) & (phase > 0))
    def _():
        da_s[r] = jnp.zeros((D, R), F32)

        @pl.when(phase == 1)
        def _():
            @pl.when(r == 0)
            def _():
                whole_dy.wait()
                h_out(NR - 2).wait()
                h_out(NR - 1).wait()
            dyt_s[:, rows] = dy_s[rows].T

        @pl.when(phase == 2)
        def _():
            keep(x_tile().astype(F32), rows)

    @pl.when(phase == 0)
    def _():
        a = a_s[rows]
        gate = dot(a, wg_s[slot])
        up = dot(a, wu_s[slot])
        h = dot((gate * sigmoid(gate) * up).astype(BF), wd_s[slot])
        da_s[r, :R] += h[:, :C]
        for i in range(4):
            da_s[r, R:, 128 * i:128 * i + 128] += h[128 * i:128 * i + 128, C:]

    @pl.when(phase >= 2)
    def _():
        pl.when((phase == 2) & (now >= 2))(lambda: by_out(now - 2).wait())

        @pl.when(phase == 3)
        def _():
            @pl.when(now == 0)
            def _():
                by_out(F * NR - 2).wait()
                by_out(F * NR - 1).wait()
                by_in(0).start()
            @pl.when(now < F * NR - 1)
            def _():
                by_in(now + 1).start()
            by_in(now).wait()

    def main(whole):
        a = a_s[rows]
        wg, wu, wd = wg_s[slot], wu_s[slot], wd_s[slot]
        gate = dot(a, wg)
        up = dot(a, wu)
        by_prod = dot_nt(dy_s[rows], wd).astype(BF).astype(F32)
        sig = sigmoid(gate)
        silu = gate * sig
        prod = (silu * up).astype(BF)
        by_up = (by_prod * silu).astype(BF)
        by_gate = (by_prod * up * (sig + silu * (1.0 - sig))).astype(BF)
        accd[...] += dot(dyt_s[:, rows], prod)
        at = at_s[:, rows]
        accg[...] += dot(at, by_gate)
        accu[...] += dot(at, by_up)
        if whole:
            da_s[r] += dot_nt(wg, by_gate) + dot_nt(wu, by_up)
        else:
            by_s[turn, 0] = by_gate
            by_s[turn, 1] = by_up
            by_out(now).start()

    @pl.when(phase == 1)
    def _():
        main(True)

    @pl.when(phase == 2)
    def _():
        main(False)

    @pl.when(phase == 3)
    def _():
        da_s[r] += dot_nt(wg_s[slot], by_s[turn, 0]) + dot_nt(wu_s[slot], by_s[turn, 1])

    def back(h):
        wide = h.astype(F32)
        scale = scale_of(wide)
        unit = wide * scale
        da = da_s[r].T
        by_wide = scale * (da - unit * jnp.mean(da * unit, -1, keepdims=True))
        return (dy_s[rows].astype(F32) + by_wide.astype(BF).astype(F32)).astype(BF)

    @pl.when(f == F - 1)
    def _():
        @pl.when(phase == 0)
        def _():
            x = x_tile().astype(F32)
            pl.when(r >= 2)(lambda: h_out(r - 2).wait())
            rest = jnp.concatenate([da_s[r, R:, 128 * i:128 * i + 128] for i in range(4)], axis=0)
            h = jnp.concatenate([da_s[r, :R], rest], axis=1)
            h1 = (x + h.astype(BF).astype(F32)).astype(BF)
            h_s[turn] = h1
            keep(h1.astype(F32), rows)
            h_out(r).start()

        @pl.when(phase == 1)
        def _():
            pl.when(r == 0)(lambda: h_in(0).start())
            pl.when(r < NR - 1)(lambda: h_in(r + 1).start())
            h_in(r).wait()
            by_h = back(h_s[turn])
            dy_s[rows] = by_h
            dyt_s[:, rows] = by_h.T

        @pl.when(phase == 3)
        def _():
            x = x_tile()
            pl.when(r >= 2)(lambda: dx_out(r - 2).wait())
            h_s[turn] = back(x)
            dx_out(r).start()

    @pl.when((q >= 0) & (q <= Q))
    def _():
        @pl.when(r < 4)
        def _():
            pl.when((r == 1) & (q >= 1) & (q < Q))(lambda: s1_load(q - 1))
            pl.when((r == 2) & (q >= 1) & (q < Q))(lambda: s1_add(q - 1))
            pl.when((r == 3) & (q >= 2))(lambda: b_load(q - 2))

        @pl.when(r >= 4)
        def _():
            pl.when((r == 4) & (q >= 2))(lambda: b_add(q - 2))
            pl.when((r == 6) & (q >= 1) & (q < Q))(lambda: s2_load(q - 1))

            @pl.when((r == 7) & (q < Q))
            def _():
                pl.when(q >= 1)(lambda: s2_add(q - 1))
                pack(q)

    @pl.when(phase == 3)
    def _():
        pl.when(now == 2)(lambda: s1_load(Q - 1))
        pl.when(now == 3)(lambda: s1_add(Q - 1))
        pl.when(now == 15)(lambda: s2_load(Q - 1))
        pl.when(now == 16)(lambda: s2_add(Q - 1))
        pl.when(now == 28)(lambda: b_load(Q - 1))
        pl.when(now == 29)(lambda: b_add(Q - 1))

        @pl.when(now == F * NR - 1)
        def _():
            dx_out(NR - 2).wait()
            dx_out(NR - 1).wait()
            s2_copy(Q - 1).wait_send()
            for last in (Q - 2, Q - 1):
                s1_copy(last, 0).wait_send()
                s1_copy(last, 1).wait_send()
                for k in range(1, NG):
                    b_copy(last, k).wait_send()
                c_sent(last)
            @pl.loop(0, Q)
            def _(each):
                for k in range(1, NG):
                    c_wait(rc_sem.at[each, k - 1])
                for way in range(3):
                    gather_wait(out_sem, each, way)


def both_passes(x, dy, weights):
    hbm = pl.BlockSpec(memory_space=pl.ANY)

    dma = pltpu.SemaphoreType.DMA
    dx, g, u, d, *_ = pl.pallas_call(
        kernel,
        grid=(4, F, NR),
        in_specs=[hbm] * 5,
        out_specs=[hbm] * 12,
        out_shape=[
            jax.ShapeDtypeStruct((T, D), BF),
            jax.ShapeDtypeStruct((2, 160, FF), BF),
            jax.ShapeDtypeStruct((2, 160, FF), BF),
            jax.ShapeDtypeStruct((2, D, D), BF),
            jax.ShapeDtypeStruct((Q, 2, BLOCK, 128), BF),
            jax.ShapeDtypeStruct((Q, BLOCK, 128), BF),
            jax.ShapeDtypeStruct((Q, NG - 1, PIECE, 128), BF),
            jax.ShapeDtypeStruct((T, D), BF),
            jax.ShapeDtypeStruct((F * NR, 2, R, C), BF),
            jax.ShapeDtypeStruct((Q, NS, 160, C), BF),
            jax.ShapeDtypeStruct((Q, NS, 160, C), BF),
            jax.ShapeDtypeStruct((Q, NS, 128, D), BF),
        ],
        scratch_shapes=[
            pltpu.VMEM((T, D), BF), pltpu.VMEM((D, T), BF), pltpu.VMEM((T, D), BF), pltpu.VMEM((D, T), BF),
            pltpu.VMEM((NR, D, R), F32),
            pltpu.VMEM((D, C), F32), pltpu.VMEM((D, C), F32), pltpu.VMEM((D, C), F32),
            pltpu.VMEM((2, D, C), BF), pltpu.VMEM((2, D, C), BF), pltpu.VMEM((2, C, D), BF),
            pltpu.VMEM((2, NS, BLOCK, 128), BF), pltpu.VMEM((BLOCK, 128), BF), pltpu.VMEM((2, NG, PIECE, 128), BF),
            pltpu.VMEM((2, 2, 80, 128), BF), pltpu.VMEM((2, 16, D), BF),
            pltpu.VMEM((2, BLOCK, 128), BF), pltpu.VMEM((BLOCK, 128), BF), pltpu.VMEM((NG - 1, PIECE, 128), BF),
            pltpu.VMEM((2, R, D), BF), pltpu.VMEM((2, R, D), BF), pltpu.VMEM((2, 2, R, C), BF),
            dma((2, 3)), dma((4,)), dma((2, 2)), dma((Q, 2)), dma((1,)), dma((Q,)), dma((2, NG - 1)), dma((Q, NG - 1)),
            dma((2, NG - 1)), dma((Q, NG - 1)), dma((2,)), dma((2,)), dma((2,)), dma((2,)), dma((3, Q)), dma((3, Q)),
        ],
        compiler_params=pltpu.CompilerParams(
            dimension_semantics=("arbitrary",) * 3, vmem_limit_bytes=63 * MB, collective_id=1, has_side_effects=True),
        cost_estimate=pl.CostEstimate(flops=38 * T * D * FF, bytes_accessed=100 * MB, transcendentals=0),
        name="both_passes",
    )(x, dy, *weights)
    return dx[None], g, u, d


def solution(mesh):
    def step(x, dy, *weights):
        return both_passes(x[0], dy[0], weights)

    states, cut = P(("rep", "r", "s"), None, None), P(None, "s", None)
    return jax.shard_map(
        step,
        mesh=mesh,
        in_specs=(states, states) + (cut,) * 3,
        out_specs=(states,) + (P("rep", "s", None),) * 3,
        check_vma=False,
    )
```

time: 508 us -> 459 us (0.904)
  Pallas kernels: 478 us -> 449 us
  local copies, waits for them, and re-layouts: 28.7 us -> 8.95 us
    pallas_call x1, Pallas kernels: 478 us -> 449 us  [both_passes(): pl.pallas_call(kernel, grid=(4, F, NR), in_specs=[hbm] * 5, out_specs=[hb...]
    reshape x3 -> x0, local copies, waits for them, and re-layouts: 8.79 us -> none  [the longest x2 5.79 us: step(): wide = lambda v: v.transpose(0, 3, 2, 1, 4).reshape(2, 160, FF)]
    unnamed x7 -> x10, local copies, waits for them, and re-layouts: 13.9 us -> 8.95 us
where the time goes in v3:
time: 459 us; the launch traced here: 458 us
  Pallas kernels  449 us (98%)
  local copies, waits for them, and re-layouts  8.95 us (2%)
    pallas_call x1, Pallas kernels, both_passes(): pl.pallas_call(kernel, grid=(4, F, NR), in_specs=[hbm] * 5, out_specs=[hb...  449 us

profile of v3, /device:TPU:0, one launch (start us, length us, event | category | flops | bytes accessed | tf_op | source)
XLA Modules:
  0.0 458.5 jit_solution(3938001387539760329)
XLA Ops:
  0.6 448.9 %both_passes.1 = (bf16[4096,640]{1,0:T(8,128)(2,1)}, bf16[2,160,2560]{2,1,0:T(8,128)(2,1)}, bf16[2,160,2560]{2,1,0:T(8,128)(2,1)}, bf16[2,640,640]{2,1,0:T(8,128...) custom-call(bf16[4096,640]{1,0:T(8,128)(2,1)} %bitcast.4, ...), custom_call_target="tpu_custom_call" | custom-call | flops 255013683200 | bytes 104857600 | tf_op jit(solution)/shard_map/both_passes/pallas_call | solution.py:476
  449.5 0.0 copy-start.2
  449.5 0.0 copy-start.1
  449.5 5.4 %copy.13 = bf16[1,4096,640]{2,1,0:T(8,128)(2,1)} copy(bf16[1,4096,640]{2,1,0:T(8,128)(2,1)} %bitcast.3) | data formatting | bytes 10485760
  455.0 0.0 copy-done.2
  455.0 0.0 copy-start
  455.0 1.2 copy.14
  456.1 0.0 copy-done.1
  456.1 1.2 copy.15
  457.3 0.0 copy-done
  457.3 1.2 copy.16
Async XLA Ops:
  449.5 5.5 %copy-start.2 = (bf16[2,160,2560]{2,1,0:T(8,128)(2,1)S(1)}, bf16[2,160,2560]{2,1,0:T(8,128)(2,1)}, u32[]{:S(2)}) copy-start(bf16[2,160,2560]{2,1,0:T(8,128)(2,1)} %get-tuple-element.17) | copy-start | bytes 4915204
  449.5 6.6 %copy-start.1 = (bf16[2,160,2560]{2,1,0:T(8,128)(2,1)S(1)}, bf16[2,160,2560]{2,1,0:T(8,128)(2,1)}, u32[]{:S(2)}) copy-start(bf16[2,160,2560]{2,1,0:T(8,128)(2,1)} %get-tuple-element.18) | copy-start | bytes 4915204
  455.0 2.3 copy-start
